TPU v7x, 32 devices: a whole 2x2x4 slice. The times are simulated.
32 devices in a mesh: seq: 2 (over y), section: 4 (over x, core), tp: 4 (over z).
Axes of the slice: x: 2, y: 2, z: 4, core: 2. Of those that a mesh axis runs over, the one named last changes fastest.
Arguments:
- token_ids: int32 [128], P('seq'), may hold values from 0 to 65535
- embed_columns: bfloat16 [4096, 65536], P(('tp', 'seq')), may hold values from -6 to 6
- norm_gain: bfloat16 [4, 4096], P('section'), may hold values from 0.099609375 to 1.8984375
- qkv_weight: bfloat16 [4, 4096, 4096], P('section', 'seq', 'tp'), may hold values from -1 to 1
- out_weight: bfloat16 [4, 4096, 2048], P('section', 'seq', 'tp'), may hold values from -0.125 to 0.125
Outputs:
- layer_states: bfloat16 [4, 128, 4096], P('section', 'seq', 'tp')
All inputs are finite; a program needn't handle non-finite values.
Results may differ from a plain program's by a relative error of at most 0.02.
Values may be sent and summed in bfloat16 or wider, within the bound.
A program may use at most 192 MiB of HBM per device.

v0:
```python
import jax
import jax.numpy as jnp
from jax import lax
from jax.sharding import PartitionSpec as P

QUERY_HEADS = 16
KEY_VALUE_HEADS = 8
HEAD_WIDTH = 128
EPS = 1e-05
ROPE_BASE = 500000.0
MASKED = -1e30


def passed_along(value, axis, steps):
    count = lax.axis_size(axis)
    leading, last = (max(0, -steps), min(count, count - steps))
    return lax.ppermute(value, axis, [(source, source + steps) for source in range(leading, last)])


def from_root(value, axis, root):
    mine = lax.axis_index(axis) == root
    return lax.psum(jnp.where(mine, value, jnp.zeros_like(value)), axis)


def rope_tables(positions, head_size):
    half_width = head_size // 2
    inverse_freq = ROPE_BASE ** (-jnp.arange(half_width).astype(jnp.float32) * (2.0 / head_size))
    angles = positions.astype(jnp.float32)[:, None] * inverse_freq[None, :]
    return (jnp.cos(angles), jnp.sin(angles))


def rotate_half(heads, cosine_table, sine_values):
    half_width = heads.shape[-1] // 2
    first_half = heads[..., :half_width]
    second = heads[..., half_width:]
    cosine_table = cosine_table[:, None, :]
    sine_values = sine_values[:, None, :]
    return jnp.concatenate(
        [
            first_half * cosine_table - second * sine_values,
            second * cosine_table + first_half * sine_values,
        ],
        axis=-1,
    )


def norm_rows(row_block, gain_row):
    values = row_block.astype(jnp.float32)
    inverse_rms = lax.rsqrt(jnp.mean(values * values, axis=-1, keepdims=True) + EPS)
    return (values * inverse_rms * gain_row[None, :]).astype(jnp.bfloat16)


def widen(current):
    return lax.all_gather(current, "tp", axis=1, tiled=True)


def project(full_rows, gain_row, qkv_full, positions, query_heads, key_value_heads):
    row_count = full_rows.shape[0]
    normed = norm_rows(full_rows, gain_row)
    projected_rows = jnp.dot(normed, qkv_full, preferred_element_type=jnp.float32)
    projected_rows = projected_rows.reshape(
        row_count, query_heads + 2 * key_value_heads, HEAD_WIDTH
    )
    cosine_table, sine_values = rope_tables(positions, HEAD_WIDTH)
    query_rows = rotate_half(projected_rows[:, :query_heads], cosine_table, sine_values).astype(
        jnp.bfloat16
    )
    key_head_rows = rotate_half(
        projected_rows[:, query_heads : query_heads + key_value_heads], cosine_table, sine_values
    ).astype(jnp.bfloat16)
    value_head_rows = projected_rows[:, query_heads + key_value_heads :].astype(jnp.bfloat16)
    return (query_rows, key_head_rows, value_head_rows)


def attend(query_rows, key_head_rows, value_head_rows, allowed):
    row_count, query_heads, head_size = query_rows.shape
    key_value_heads = key_head_rows.shape[1]
    query_groups = query_rows.reshape(
        row_count, key_value_heads, query_heads // key_value_heads, head_size
    )
    scores = jnp.einsum(
        "rkph,ckh->kprc", query_groups, key_head_rows, preferred_element_type=jnp.float32
    ) * head_size ** (-0.5)
    scores = jnp.where(allowed[None, None], scores, MASKED)
    weights = jax.nn.softmax(scores, axis=-1).astype(jnp.bfloat16)
    attended = jnp.einsum(
        "kprc,ckh->rkph", weights, value_head_rows, preferred_element_type=jnp.float32
    )
    return attended.reshape(row_count, query_heads * head_size).astype(jnp.bfloat16)


def combine(current, attended, out_full):
    partial_value = lax.dot_general(
        attended, out_full, (((1,), (1,)), ((), ())), preferred_element_type=jnp.float32
    )
    summed = lax.psum_scatter(
        partial_value.astype(jnp.bfloat16), "tp", scatter_dimension=1, tiled=True
    ).astype(jnp.float32)
    return (current.astype(jnp.float32) + summed).astype(jnp.bfloat16)


def advance(new_rows):
    return passed_along(new_rows, "section", 1)


def body(token_ids, embed_columns, norm_gain, qkv_weight, out_weight):
    seq_count = lax.axis_size("seq")
    section_count = lax.axis_size("section")
    tensor_parallel_count = lax.axis_size("tp")
    group_index = lax.axis_index("seq")
    section_index = lax.axis_index("section")
    block_row_slice = token_ids.shape[0]
    feature_slice = embed_columns.shape[0]
    feature_cols = feature_slice * seq_count
    query_heads = QUERY_HEADS // tensor_parallel_count
    key_value_heads = KEY_VALUE_HEADS // tensor_parallel_count
    every_id = lax.all_gather(token_ids, "seq", axis=0, tiled=True)
    looked = jnp.take(embed_columns, every_id, axis=1)
    arrived = lax.all_to_all(looked, "seq", split_axis=1, concat_axis=0, tiled=True)
    residual = arrived.T
    qkv_full, out_full = (
        lax.all_gather(qkv_weight, "seq", axis=1, tiled=True),
        lax.all_gather(out_weight, "seq", axis=1, tiled=True),
    )
    qkv_full = qkv_full[0]
    out_full = out_full[0]
    gain_row = norm_gain[0].astype(jnp.float32)
    outputs = jnp.zeros((block_row_slice, feature_cols), jnp.bfloat16)
    row_ids = jnp.arange(block_row_slice)[:, None]
    column = jnp.arange(2 * block_row_slice)[None, :]
    positions = group_index * block_row_slice + jnp.arange(block_row_slice)
    allowed = jnp.where(
        column < block_row_slice, group_index > 0, column - block_row_slice <= row_ids
    )
    current = residual
    for step_number in range(section_count):
        query_rows, key_head_rows, value_head_rows = project(
            widen(current), gain_row, qkv_full, positions, query_heads, key_value_heads
        )
        anchor_heads, anchor_values = (
            from_root(key_head_rows, "seq", 0),
            from_root(value_head_rows, "seq", 0),
        )
        both_keys = jnp.concatenate([anchor_heads, key_head_rows], axis=0)
        both_values = jnp.concatenate([anchor_values, value_head_rows], axis=0)
        attended = attend(query_rows, both_keys, both_values, allowed)
        new_rows = combine(current, attended, out_full)
        outputs = jnp.where(section_index == step_number, new_rows, outputs)
        if step_number + 1 < section_count:
            current = advance(new_rows)
    return outputs[None]


def solution(mesh):
    placed = (
        P("seq"),
        P(("tp", "seq"), None),
        P("section", None),
        P("section", "seq", "tp"),
        P("section", "seq", "tp"),
    )
    return jax.shard_map(
        body, mesh=mesh, in_specs=placed, out_specs=P("section", "seq", "tp"), check_vma=False
    )
```

profile of v0, /device:TPU:0, one launch (start us, length us, event | category | flops | bytes accessed | tf_op | source)
XLA Modules:
  0.0 499.6 jit_solution(5250696001412698357)
XLA Ops:
  7.3 87.1 %copy.18 = bf16[512,65536]{0,1:T(8,128)(2,1)} copy(bf16[512,65536]{1,0:T(8,128)(2,1)} %param.6) | data formatting | bytes 134217728 | tf_op args[1]
  95.9 5.4 %all-reduce = s32[128]{0:T(128)S(1)} all-reduce(s32[128]{0:T(128)S(1)} %dynamic-update-slice), channel_id=1, replica_groups=mesh['seq'=2,'section'=4,'tp'=4] {'seq'}, use_global_device_ids=true, to_apply=%add | all-reduce | flops 128 | bytes 1024
  101.4 2.0 gather_fusion
  104.2 3.4 all-to-all-start
  107.9 5.7 %all-to-all-done = bf16[512,2,64]{0,2,1:T(8,128)(2,1)S(1)} async-done(((bf16[512,2,64]{0,2,1:T(8,128)(2,1)}), bf16[512,2,64]{0,2,1:T(8,128)(2,1)S(1)}, u32[]{:S(2)}, u32[]{:S(2)}) %all-to-all-start) | async-done | bytes 131104 | tf_op jit(solution)/shard_map/all_to_all | solution.py:119
  113.7 15.8 %all_gather.22 = bf16[64,4096]{1,0:T(8,128)(2,1)S(1)} all-gather(bf16[64,1024]{1,0:T(8,128)(2,1)S(1)} %bitcast.203), channel_id=1, replica_groups=mesh['seq'=2,'section'=4,'tp'=4] {'tp'}, dimensions={1}, use_global_device_ids=true | all-gather | bytes 655360 | tf_op jit(solution)/shard_map/all_gather | solution.py:54
  129.7 11.3 %copy.20 = bf16[1024,4096]{1,0:T(8,128)(2,1)} copy(bf16[1024,4096]{0,1:T(8,128)(2,1)} %bitcast.202) | data formatting | bytes 16777216 | tf_op jit(solution)/shard_map/dot_general | solution.py:60
  141.0 6.0 %fusion.50 = f32[64,8,128]{2,0,1:T(8,128)S(1)} fusion(bf16[8,128,4096]{2,1,0:T(8,128)(2,1)} %bitcast.198, bf16[64,4096]{1,0:T(8,128)(2,1)S(1)} %all_gather.22, f32[4096]{0:T(1024)S(1)} %bitcast.207, f32[64]{0:T(128)S(1)} %add_rsqrt_fusion.3), kind=kOutput, calls=%fused_computation.68 | convolution fusion | flops 537919488 | bytes 9191680 | tf_op jit(solution)/shard_map/dot_general | solution.py:60
  148.8 20.2 %all-reduce.16.cloned.1.call-done = (bf16[64,2,128]{2,0,1:T(8,128)(2,1)}, bf16[64,2,128]{2,0,1:T(8,128)(2,1)}) async-done(((bf16[64,2,128]{2,0,1:T(8,128)(2,1)}, bf16[64,2,128]{2,0,1:T(8,128)(2,1)}), (bf16[64,2,128]{2,0,1:T(8,128)(2,1)}, bf16[64,2,128]{2,0,1:T(8,128)(2,1)})) %all-reduce.16.cloned.1.call-update) | async-done | bytes 65552 | tf_op jit(solution)/shard_map/psum | solution.py:22
  170.2 1.4 fusion.24
  171.7 55.7 %all-gather.5.cloned.1.call-done = bf16[1,4096,512]{2,1,0:T(8,128)(2,1)} async-done(((bf16[1,2048,512]{2,1,0:T(8,128)(2,1)}), bf16[1,4096,512]{2,1,0:T(8,128)(2,1)}) %all-gather.5.cloned.1.call-update) | async-done | bytes 4194320 | tf_op jit(solution)/shard_map/all_gather | solution.py:123
  227.3 4.4 convolution_convert_fusion.3
  231.8 22.0 %reduce-scatter.5.cloned.1.call-done = bf16[64,1024]{1,0:T(8,128)(2,1)} async-done(((bf16[64,4096]{1,0:T(8,128)(2,1)}), bf16[64,1024]{1,0:T(8,128)(2,1)}) %reduce-scatter.5.cloned.1.call-update) | async-done | bytes 131088 | tf_op jit(solution)/shard_map/reduce_scatter | solution.py:96
  257.0 15.0 %all_gather.25 = bf16[64,4096]{1,0:T(8,128)(2,1)S(1)} all-gather(bf16[64,1024]{1,0:T(8,128)(2,1)S(1)} %collective-permute-done), channel_id=1, replica_groups=mesh['seq'=2,'section'=4,'tp'=4] {'tp'}, dimensions={1}, use_global_device_ids=true | all-gather | bytes 655360 | tf_op jit(solution)/shard_map/all_gather | solution.py:54
  272.2 6.1 %fusion.47 = f32[64,8,128]{2,0,1:T(8,128)S(1)} fusion(bf16[8,128,4096]{2,1,0:T(8,128)(2,1)} %bitcast.199, bf16[64,4096]{1,0:T(8,128)(2,1)S(1)} %all_gather.25, f32[64]{0:T(128)S(1)} %add_rsqrt_fusion.2, f32[4096]{0:T(1024)S(1)} %bitcast.208), kind=kOutput, calls=%fused_computation.66 | convolution fusion | flops 537919488 | bytes 9191680 | tf_op jit(solution)/shard_map/dot_general | solution.py:60
  279.9 23.9 %all-reduce.14.cloned.1.call-done = (bf16[64,2,128]{2,0,1:T(8,128)(2,1)}, bf16[64,2,128]{2,0,1:T(8,128)(2,1)}) async-done(((bf16[64,2,128]{2,0,1:T(8,128)(2,1)}, bf16[64,2,128]{2,0,1:T(8,128)(2,1)}), (bf16[64,2,128]{2,0,1:T(8,128)(2,1)}, bf16[64,2,128]{2,0,1:T(8,128)(2,1)})) %all-reduce.14.cloned.1.call-update) | async-done | bytes 65552 | tf_op jit(solution)/shard_map/psum | solution.py:22
  305.0 1.4 fusion.25
  306.4 4.4 convolution_convert_fusion.2
  310.9 22.0 %reduce-scatter.7.cloned.1.call-done = bf16[64,1024]{1,0:T(8,128)(2,1)} async-done(((bf16[64,4096]{1,0:T(8,128)(2,1)}), bf16[64,1024]{1,0:T(8,128)(2,1)}) %reduce-scatter.7.cloned.1.call-update) | async-done | bytes 131088 | tf_op jit(solution)/shard_map/reduce_scatter | solution.py:96
  336.1 15.2 %all_gather.26 = bf16[64,4096]{1,0:T(8,128)(2,1)S(1)} all-gather(bf16[64,1024]{1,0:T(8,128)(2,1)S(1)} %collective-permute-done.1), channel_id=1, replica_groups=mesh['seq'=2,'section'=4,'tp'=4] {'tp'}, dimensions={1}, use_global_device_ids=true | all-gather | bytes 655360 | tf_op jit(solution)/shard_map/all_gather | solution.py:54
  351.5 6.1 %fusion.44 = f32[64,8,128]{2,0,1:T(8,128)S(1)} fusion(bf16[8,128,4096]{2,1,0:T(8,128)(2,1)} %bitcast.200, bf16[64,4096]{1,0:T(8,128)(2,1)S(1)} %all_gather.26, f32[64]{0:T(128)S(1)} %add_rsqrt_fusion.1, f32[4096]{0:T(1024)S(1)} %bitcast.209), kind=kOutput, calls=%fused_computation.64 | convolution fusion | flops 537919488 | bytes 9191680 | tf_op jit(solution)/shard_map/dot_general | solution.py:60
  359.2 23.9 %all-reduce.12.cloned.1.call-done = (bf16[64,2,128]{2,0,1:T(8,128)(2,1)}, bf16[64,2,128]{2,0,1:T(8,128)(2,1)}) async-done(((bf16[64,2,128]{2,0,1:T(8,128)(2,1)}, bf16[64,2,128]{2,0,1:T(8,128)(2,1)}), (bf16[64,2,128]{2,0,1:T(8,128)(2,1)}, bf16[64,2,128]{2,0,1:T(8,128)(2,1)})) %all-reduce.12.cloned.1.call-update) | async-done | bytes 65552 | tf_op jit(solution)/shard_map/psum | solution.py:22
  384.2 1.4 fusion.26
  385.7 4.4 convolution_convert_fusion.1
  390.2 22.0 %reduce-scatter.9.cloned.1.call-done = bf16[64,1024]{1,0:T(8,128)(2,1)} async-done(((bf16[64,4096]{1,0:T(8,128)(2,1)}), bf16[64,1024]{1,0:T(8,128)(2,1)}) %reduce-scatter.9.cloned.1.call-update) | async-done | bytes 131088 | tf_op jit(solution)/shard_map/reduce_scatter | solution.py:96
  415.4 15.1 %all_gather.27 = bf16[64,4096]{1,0:T(8,128)(2,1)S(1)} all-gather(bf16[64,1024]{1,0:T(8,128)(2,1)S(1)} %collective-permute-done.2), channel_id=1, replica_groups=mesh['seq'=2,'section'=4,'tp'=4] {'tp'}, dimensions={1}, use_global_device_ids=true | all-gather | bytes 655360 | tf_op jit(solution)/shard_map/all_gather | solution.py:54
  430.6 6.1 %fusion.41 = f32[64,8,128]{2,0,1:T(8,128)S(1)} fusion(bf16[8,128,4096]{2,1,0:T(8,128)(2,1)} %bitcast.201, bf16[64,4096]{1,0:T(8,128)(2,1)S(1)} %all_gather.27, f32[64]{0:T(128)S(1)} %add_rsqrt_fusion, f32[4096]{0:T(1024)S(1)} %bitcast.210), kind=kOutput, calls=%fused_computation.62 | convolution fusion | flops 537919488 | bytes 9191680 | tf_op jit(solution)/shard_map/dot_general | solution.py:60
  438.3 23.9 %all-reduce.10.cloned.1.call-done = (bf16[64,2,128]{2,0,1:T(8,128)(2,1)}, bf16[64,2,128]{2,0,1:T(8,128)(2,1)}) async-done(((bf16[64,2,128]{2,0,1:T(8,128)(2,1)}, bf16[64,2,128]{2,0,1:T(8,128)(2,1)}), (bf16[64,2,128]{2,0,1:T(8,128)(2,1)}, bf16[64,2,128]{2,0,1:T(8,128)(2,1)})) %all-reduce.10.cloned.1.call-update) | async-done | bytes 65552 | tf_op jit(solution)/shard_map/psum | solution.py:22
  463.3 1.4 fusion.27
  464.8 4.4 convolution_convert_fusion
  469.2 22.0 %reduce-scatter.11.cloned.1.call-done = bf16[64,1024]{1,0:T(8,128)(2,1)} async-done(((bf16[64,4096]{1,0:T(8,128)(2,1)}), bf16[64,1024]{1,0:T(8,128)(2,1)}) %reduce-scatter.11.cloned.1.call-update) | async-done | bytes 131088 | tf_op jit(solution)/shard_map/reduce_scatter | solution.py:96
  491.2 1.6 fusion.61
  (87 shorter events, 24.9 us)
Async XLA Ops:
  6.5 123.2 %all-gather.3.cloned.1.call-start = ((), (), s32[]{:S(2)}) async-start(), calls=%async_computation.5 | async-start | bytes 12582912 | tf_op jit(solution)/shard_map/all_gather | solution.py:122
  7.3 87.1 %copy-start.2 = (u32[32]{0:T(128)S(1)}, u32[32]{0:T(128)}, u32[]{:S(2)}) copy-start(u32[32]{0:T(128)} %constant.68) | copy-start | bytes 388
  7.3 88.4 %copy-start.1 = (s32[64]{0:T(128)S(1)}, s32[64]{0:T(128)}, u32[]{:S(2)}) copy-start(s32[64]{0:T(128)} %param.5) | copy-start | bytes 772
  7.3 100.6 %copy-start = (bf16[1,4096]{1,0:T(2,128)(2,1)S(1)}, bf16[1,4096]{1,0:T(2,128)(2,1)}, u32[]{:S(2)}) copy-start(bf16[1,4096]{1,0:T(2,128)(2,1)} %param.7) | copy-start | bytes 24580
  104.2 9.5 %all-to-all-start = ((bf16[512,2,64]{0,2,1:T(8,128)(2,1)}), bf16[512,2,64]{0,2,1:T(8,128)(2,1)S(1)}, u32[]{:S(2)}, u32[]{:S(2)}) async-start(bf16[512,2,64]{0,2,1:T(8,128)(2,1)} %broadcast_select_fusion), calls=%async_computation | async-start | bytes 262144 | tf_op jit(solution)/shard_map/all_to_all | solution.py:119
  107.6 61.5 %all-reduce.16.cloned.1.call-start = ((), (), s32[]{:S(2)}) async-start(), calls=%async_computation.14 | async-start | bytes 131072 | tf_op jit(solution)/shard_map/psum | solution.py:22
  147.9 79.5 %all-gather.5.cloned.1.call-start = ((), (), s32[]{:S(2)}) async-start(), calls=%async_computation.6 | async-start | bytes 6291456 | tf_op jit(solution)/shard_map/all_gather | solution.py:123
  148.6 105.2 %reduce-scatter.5.cloned.1.call-start = ((), (), s32[]{:S(2)}) async-start(), calls=%async_computation.7 | async-start | bytes 655360 | tf_op jit(solution)/shard_map/reduce_scatter | solution.py:96
  231.8 72.0 %all-reduce.14.cloned.1.call-start = ((), (), s32[]{:S(2)}) async-start(), calls=%async_computation.13 | async-start | bytes 131072 | tf_op jit(solution)/shard_map/psum | solution.py:22
  254.7 2.3 collective-permute-start
  279.7 53.1 %reduce-scatter.7.cloned.1.call-start = ((), (), s32[]{:S(2)}) async-start(), calls=%async_computation.8 | async-start | bytes 655360 | tf_op jit(solution)/shard_map/reduce_scatter | solution.py:96
  310.9 72.2 %all-reduce.12.cloned.1.call-start = ((), (), s32[]{:S(2)}) async-start(), calls=%async_computation.12 | async-start | bytes 131072 | tf_op jit(solution)/shard_map/psum | solution.py:22
  333.8 2.3 collective-permute-start.1
  359.0 53.1 %reduce-scatter.9.cloned.1.call-start = ((), (), s32[]{:S(2)}) async-start(), calls=%async_computation.9 | async-start | bytes 655360 | tf_op jit(solution)/shard_map/reduce_scatter | solution.py:96
  390.1 72.0 %all-reduce.10.cloned.1.call-start = ((), (), s32[]{:S(2)}) async-start(), calls=%async_computation.11 | async-start | bytes 131072 | tf_op jit(solution)/shard_map/psum | solution.py:22
  413.1 2.3 collective-permute-start.2
  438.1 53.1 %reduce-scatter.11.cloned.1.call-start = ((), (), s32[]{:S(2)}) async-start(), calls=%async_computation.10 | async-start | bytes 655360 | tf_op jit(solution)/shard_map/reduce_scatter | solution.py:96
Sparse Core Ops, SparseCore 0:
  8.9 108.1 all-gather.2
  148.0 21.0 all-reduce.15
  170.6 56.7 all-gather.4
  231.9 21.8 reduce-scatter.4
  279.8 23.8 all-reduce.13
  311.0 21.8 reduce-scatter.6
  359.1 23.8 all-reduce.11
  390.3 21.8 reduce-scatter.8
  438.2 23.8 all-reduce.9
  469.3 21.8 reduce-scatter.10
where the time goes:
time: 503 us; the launch traced here: 500 us
  waiting for transfers between devices  246 us (49%)
  local copies, waits for them, and re-layouts  102 us (20%)
  blocking collectives  66.5 us (13%)
  matrix products  51.9 us (10%)
  between operations  14.5 us (3%)
  other arithmetic  11.7 us (2%)
  starting transfers between devices  7.64 us (2%)
    psum x4, waiting for transfers between devices, from_root(): return lax.psum(jnp.where(mine, value, jnp.zeros_like(value)), axis)  91.9 us
    unnamed x10, local copies, waits for them, and re-layouts  87.9 us
    reduce_scatter x4, waiting for transfers between devices, combine(): lax.psum_scatter(partial_value.astype(jnp.bfloat16), 'tp', scatter_dimens...  87.9 us
    all_gather x4, blocking collectives, widen(): return lax.all_gather(current, 'tp', axis=1, tiled=True)  61.1 us
    all_gather x1, waiting for transfers between devices, body(): lax.all_gather(out_weight, 'seq', axis=1, tiled=True)  55.7 us
    dot_general x4, matrix products, project(): jnp.dot(normed, qkv_full, preferred_element_type=jnp.float32)  24.2 us
    dot_general x4, matrix products, combine(): lax.dot_general(attended, out_full, (((1,), (1,)), ((), ())), preferred_e...  17.5 us
    dot_general x1, local copies, waits for them, and re-layouts, project(): jnp.dot(normed, qkv_full, preferred_element_type=jnp.float32)  11.3 us
  transfers between devices with their start and end apart: 14, of which 13 were waited for; matrix products, arithmetic and copies ran while one was open for 19% of the time, Pallas kernels for 0%

commit v1 on v0

--- a/solution.py
+++ b/solution.py
@@ -19,7 +19,7 @@
 
 def from_root(value, axis, root):
     mine = lax.axis_index(axis) == root
-    return lax.psum(jnp.where(mine, value, jnp.zeros_like(value)), axis)
+    return jnp.sum(lax.all_gather(jnp.where(mine, value, jnp.zeros_like(value)), axis), axis=0)
 
 
 def rope_tables(positions, head_size):

time: 503 us -> 409 us (0.81)
  waiting for transfers between devices: 246 us -> 123 us
  blocking collectives: 66.5 us -> 106 us
  matrix products: 51.9 us -> 45.9 us
    psum x4 -> x0, waiting for transfers between devices: 91.9 us -> none  [from_root(): return lax.psum(jnp.where(mine, value, jnp.zeros_like(value)), axis)]
    all_gather x1, waiting for transfers between devices: 55.7 us -> 16.4 us  [body(): lax.all_gather(out_weight, 'seq', axis=1, tiled=True)]
    all_gather x0 -> x8, blocking collectives: none -> 39 us  [from_root(): lax.all_gather(jnp.where(mine, value, jnp.zeros_like(value)), axis)]
    reduce_scatter x4, waiting for transfers between devices: 87.9 us -> 96.2 us  [combine(): lax.psum_scatter(partial_value.astype(jnp.bfloat16), 'tp', scatter_dimens...]
  transfers between devices with their start and end apart: 14 -> 10, of which waited for: 13 -> 9; matrix products, arithmetic and copies ran while one was open for 19% -> 27% of each run, Pallas kernels for 0% -> 0%
where the time goes in v1:
time: 409 us; the launch traced here: 406 us
  waiting for transfers between devices  123 us (30%)
  blocking collectives  106 us (26%)
  local copies, waits for them, and re-layouts  102 us (25%)
  matrix products  45.9 us (11%)
  between operations  14.5 us (4%)
  other arithmetic  7.6 us (2%)
  starting transfers between devices  7.48 us (2%)
    reduce_scatter x4, waiting for transfers between devices, combine(): lax.psum_scatter(partial_value.astype(jnp.bfloat16), 'tp', scatter_dimens...  96.2 us
    unnamed x10, local copies, waits for them, and re-layouts  87.9 us
    all_gather x4, blocking collectives, widen(): return lax.all_gather(current, 'tp', axis=1, tiled=True)  61.1 us
    all_gather x8, blocking collectives, from_root(): lax.all_gather(jnp.where(mine, value, jnp.zeros_like(value)), axis)  39 us
    dot_general x4, matrix products, project(): jnp.dot(normed, qkv_full, preferred_element_type=jnp.float32)  24.2 us
    dot_general x4, matrix products, combine(): lax.dot_general(attended, out_full, (((1,), (1,)), ((), ())), preferred_e...  17.6 us
    all_gather x1, waiting for transfers between devices, body(): lax.all_gather(out_weight, 'seq', axis=1, tiled=True)  16.4 us
    dot_general x1, local copies, waits for them, and re-layouts, project(): jnp.dot(normed, qkv_full, preferred_element_type=jnp.float32)  11.4 us
  transfers between devices with their start and end apart: 10, of which 9 were waited for; matrix products, arithmetic and copies ran while one was open for 27% of the time, Pallas kernels for 0%

profile of v1, /device:TPU:0, one launch (start us, length us, event | category | flops | bytes accessed | tf_op | source)
XLA Modules:
  0.0 405.5 jit_solution(10245588875366697016)
XLA Ops:
  8.0 87.1 %copy.18 = bf16[512,65536]{0,1:T(8,128)(2,1)} copy(bf16[512,65536]{1,0:T(8,128)(2,1)} %param.6) | data formatting | bytes 134217728 | tf_op args[1]
  96.6 5.5 %all-reduce = s32[128]{0:T(128)S(1)} all-reduce(s32[128]{0:T(128)S(1)} %dynamic-update-slice), channel_id=1, replica_groups=mesh['seq'=2,'section'=4,'tp'=4] {'seq'}, use_global_device_ids=true, to_apply=%add | all-reduce | flops 128 | bytes 1024
  102.2 2.0 gather_fusion
  105.0 3.4 all-to-all-start
  108.7 5.7 %all-to-all-done = bf16[512,2,64]{0,2,1:T(8,128)(2,1)S(1)} async-done(((bf16[512,2,64]{0,2,1:T(8,128)(2,1)}), bf16[512,2,64]{0,2,1:T(8,128)(2,1)S(1)}, u32[]{:S(2)}, u32[]{:S(2)}) %all-to-all-start) | async-done | bytes 131104 | tf_op jit(solution)/shard_map/all_to_all | solution.py:119
  114.4 15.6 %all_gather.62 = bf16[64,4096]{1,0:T(8,128)(2,1)S(1)} all-gather(bf16[64,1024]{1,0:T(8,128)(2,1)S(1)} %bitcast.215), channel_id=1, replica_groups=mesh['seq'=2,'section'=4,'tp'=4] {'tp'}, dimensions={1}, use_global_device_ids=true | all-gather | bytes 655360 | tf_op jit(solution)/shard_map/all_gather | solution.py:54
  130.3 11.4 %copy.20 = bf16[1024,4096]{1,0:T(8,128)(2,1)} copy(bf16[1024,4096]{0,1:T(8,128)(2,1)} %bitcast.214) | data formatting | bytes 16777216 | tf_op jit(solution)/shard_map/dot_general | solution.py:60
  141.7 6.0 %fusion.50 = f32[64,8,128]{2,0,1:T(8,128)S(1)} fusion(bf16[8,128,4096]{2,1,0:T(8,128)(2,1)} %bitcast.210, bf16[64,4096]{1,0:T(8,128)(2,1)S(1)} %all_gather.62, f32[4096]{0:T(1024)S(1)} %bitcast.219, f32[64]{0:T(128)S(1)} %add_rsqrt_fusion.3), kind=kOutput, calls=%fused_computation.68 | convolution fusion | flops 537919488 | bytes 9191680 | tf_op jit(solution)/shard_map/dot_general | solution.py:60
  147.9 5.8 %all_gather.66 = bf16[2,64,2,128]{3,1,2,0:T(8,128)(2,1)S(1)} all-gather(bf16[1,64,2,128]{3,1,2,0:T(8,128)(2,1)S(1)} %maximum_select_fusion), channel_id=1, replica_groups=mesh['seq'=2,'section'=4,'tp'=4] {'seq'}, dimensions={0}, use_global_device_ids=true | all-gather | bytes 98304 | tf_op jit(solution)/shard_map/all_gather | solution.py:22
  153.7 5.4 %all-gather = bf16[128,2,128]{2,0,1:T(8,128)(2,1)S(1)} all-gather(bf16[64,2,128]{2,0,1:T(8,128)(2,1)S(1)} %get-tuple-element.11), channel_id=2, replica_groups=mesh['seq'=2,'section'=4,'tp'=4] {'seq'}, dimensions={0}, use_global_device_ids=true | all-gather | bytes 98304 | tf_op jit(solution)/shard_map/all_gather | solution.py:22
  160.4 16.4 %all-gather.9.cloned.1.call-done = bf16[1,4096,512]{2,1,0:T(8,128)(2,1)} async-done(((bf16[1,2048,512]{2,1,0:T(8,128)(2,1)}), bf16[1,4096,512]{2,1,0:T(8,128)(2,1)}) %all-gather.9.cloned.1.call-update) | async-done | bytes 4194320 | tf_op jit(solution)/shard_map/all_gather | solution.py:123
  176.8 4.4 %convolution_convert_fusion.3 = bf16[64,4096]{1,0:T(8,128)(2,1)} fusion(bf16[64,512]{1,0:T(8,128)(2,1)S(1)} %convert_element_type.210, bf16[1,4096,512]{2,1,0:T(8,128)(2,1)} %all-gather.9.cloned.1.call-done), kind=kOutput, calls=%fused_computation.8 | convolution fusion | flops 268697600 | bytes 4784128 | tf_op jit(solution)/shard_map/dot_general | solution.py:93
  181.3 22.0 %reduce-scatter.5.cloned.1.call-done = bf16[64,1024]{1,0:T(8,128)(2,1)} async-done(((bf16[64,4096]{1,0:T(8,128)(2,1)}), bf16[64,1024]{1,0:T(8,128)(2,1)}) %reduce-scatter.5.cloned.1.call-update) | async-done | bytes 131088 | tf_op jit(solution)/shard_map/reduce_scatter | solution.py:96
  206.5 15.1 %all_gather.68 = bf16[64,4096]{1,0:T(8,128)(2,1)S(1)} all-gather(bf16[64,1024]{1,0:T(8,128)(2,1)S(1)} %collective-permute-done), channel_id=1, replica_groups=mesh['seq'=2,'section'=4,'tp'=4] {'tp'}, dimensions={1}, use_global_device_ids=true | all-gather | bytes 655360 | tf_op jit(solution)/shard_map/all_gather | solution.py:54
  221.7 6.1 %fusion.47 = f32[64,8,128]{2,0,1:T(8,128)S(1)} fusion(bf16[8,128,4096]{2,1,0:T(8,128)(2,1)} %bitcast.211, bf16[64,4096]{1,0:T(8,128)(2,1)S(1)} %all_gather.68, f32[64]{0:T(128)S(1)} %add_rsqrt_fusion.2, f32[4096]{0:T(1024)S(1)} %bitcast.220), kind=kOutput, calls=%fused_computation.66 | convolution fusion | flops 537919488 | bytes 9191680 | tf_op jit(solution)/shard_map/dot_general | solution.py:60
  228.1 4.6 %all_gather.71 = bf16[2,64,2,128]{3,1,2,0:T(8,128)(2,1)S(1)} all-gather(bf16[1,64,2,128]{3,1,2,0:T(8,128)(2,1)S(1)} %maximum_select_fusion.1), channel_id=1, replica_groups=mesh['seq'=2,'section'=4,'tp'=4] {'seq'}, dimensions={0}, use_global_device_ids=true | all-gather | bytes 98304 | tf_op jit(solution)/shard_map/all_gather | solution.py:22
  232.7 4.7 %all-gather.1 = bf16[128,2,128]{2,0,1:T(8,128)(2,1)S(1)} all-gather(bf16[64,2,128]{2,0,1:T(8,128)(2,1)S(1)} %get-tuple-element.9), channel_id=3, replica_groups=mesh['seq'=2,'section'=4,'tp'=4] {'seq'}, dimensions={0}, use_global_device_ids=true | all-gather | bytes 98304 | tf_op jit(solution)/shard_map/all_gather | solution.py:22
  238.5 4.4 %convolution_convert_fusion.2 = bf16[64,4096]{1,0:T(8,128)(2,1)} fusion(bf16[64,512]{1,0:T(8,128)(2,1)S(1)} %convert_element_type.220, bf16[1,4096,512]{2,1,0:T(8,128)(2,1)} %all-gather.9.cloned.1.call-done), kind=kOutput, calls=%fused_computation.7 | convolution fusion | flops 268697600 | bytes 4784128 | tf_op jit(solution)/shard_map/dot_general | solution.py:93
  243.0 24.7 %reduce-scatter.7.cloned.1.call-done = bf16[64,1024]{1,0:T(8,128)(2,1)} async-done(((bf16[64,4096]{1,0:T(8,128)(2,1)}), bf16[64,1024]{1,0:T(8,128)(2,1)}) %reduce-scatter.7.cloned.1.call-update) | async-done | bytes 131088 | tf_op jit(solution)/shard_map/reduce_scatter | solution.py:96
  271.0 15.2 %all_gather.72 = bf16[64,4096]{1,0:T(8,128)(2,1)S(1)} all-gather(bf16[64,1024]{1,0:T(8,128)(2,1)S(1)} %collective-permute-done.1), channel_id=1, replica_groups=mesh['seq'=2,'section'=4,'tp'=4] {'tp'}, dimensions={1}, use_global_device_ids=true | all-gather | bytes 655360 | tf_op jit(solution)/shard_map/all_gather | solution.py:54
  286.4 6.1 %fusion.44 = f32[64,8,128]{2,0,1:T(8,128)S(1)} fusion(bf16[8,128,4096]{2,1,0:T(8,128)(2,1)} %bitcast.212, bf16[64,4096]{1,0:T(8,128)(2,1)S(1)} %all_gather.72, f32[64]{0:T(128)S(1)} %add_rsqrt_fusion.1, f32[4096]{0:T(1024)S(1)} %bitcast.221), kind=kOutput, calls=%fused_computation.64 | convolution fusion | flops 537919488 | bytes 9191680 | tf_op jit(solution)/shard_map/dot_general | solution.py:60
  292.8 4.6 %all_gather.75 = bf16[2,64,2,128]{3,1,2,0:T(8,128)(2,1)S(1)} all-gather(bf16[1,64,2,128]{3,1,2,0:T(8,128)(2,1)S(1)} %maximum_select_fusion.2), channel_id=1, replica_groups=mesh['seq'=2,'section'=4,'tp'=4] {'seq'}, dimensions={0}, use_global_device_ids=true | all-gather | bytes 98304 | tf_op jit(solution)/shard_map/all_gather | solution.py:22
  297.4 4.7 %all-gather.2 = bf16[128,2,128]{2,0,1:T(8,128)(2,1)S(1)} all-gather(bf16[64,2,128]{2,0,1:T(8,128)(2,1)S(1)} %get-tuple-element.7), channel_id=4, replica_groups=mesh['seq'=2,'section'=4,'tp'=4] {'seq'}, dimensions={0}, use_global_device_ids=true | all-gather | bytes 98304 | tf_op jit(solution)/shard_map/all_gather | solution.py:22
  303.3 4.4 %convolution_convert_fusion.1 = bf16[64,4096]{1,0:T(8,128)(2,1)} fusion(bf16[64,512]{1,0:T(8,128)(2,1)S(1)} %convert_element_type.230, bf16[1,4096,512]{2,1,0:T(8,128)(2,1)} %all-gather.9.cloned.1.call-done), kind=kOutput, calls=%fused_computation.6 | convolution fusion | flops 268697600 | bytes 4784128 | tf_op jit(solution)/shard_map/dot_general | solution.py:93
  307.8 24.7 %reduce-scatter.9.cloned.1.call-done = bf16[64,1024]{1,0:T(8,128)(2,1)} async-done(((bf16[64,4096]{1,0:T(8,128)(2,1)}), bf16[64,1024]{1,0:T(8,128)(2,1)}) %reduce-scatter.9.cloned.1.call-update) | async-done | bytes 131088 | tf_op jit(solution)/shard_map/reduce_scatter | solution.py:96
  335.7 15.1 %all_gather.76 = bf16[64,4096]{1,0:T(8,128)(2,1)S(1)} all-gather(bf16[64,1024]{1,0:T(8,128)(2,1)S(1)} %collective-permute-done.2), channel_id=1, replica_groups=mesh['seq'=2,'section'=4,'tp'=4] {'tp'}, dimensions={1}, use_global_device_ids=true | all-gather | bytes 655360 | tf_op jit(solution)/shard_map/all_gather | solution.py:54
  351.1 6.1 %fusion.41 = f32[64,8,128]{2,0,1:T(8,128)S(1)} fusion(bf16[8,128,4096]{2,1,0:T(8,128)(2,1)} %bitcast.213, bf16[64,4096]{1,0:T(8,128)(2,1)S(1)} %all_gather.76, f32[64]{0:T(128)S(1)} %add_rsqrt_fusion, f32[4096]{0:T(1024)S(1)} %bitcast.222), kind=kOutput, calls=%fused_computation.62 | convolution fusion | flops 537919488 | bytes 9191680 | tf_op jit(solution)/shard_map/dot_general | solution.py:60
  357.5 4.6 %all_gather.79 = bf16[2,64,2,128]{3,1,2,0:T(8,128)(2,1)S(1)} all-gather(bf16[1,64,2,128]{3,1,2,0:T(8,128)(2,1)S(1)} %maximum_select_fusion.3), channel_id=1, replica_groups=mesh['seq'=2,'section'=4,'tp'=4] {'seq'}, dimensions={0}, use_global_device_ids=true | all-gather | bytes 98304 | tf_op jit(solution)/shard_map/all_gather | solution.py:22
  362.1 4.7 %all-gather.3 = bf16[128,2,128]{2,0,1:T(8,128)(2,1)S(1)} all-gather(bf16[64,2,128]{2,0,1:T(8,128)(2,1)S(1)} %get-tuple-element.5), channel_id=5, replica_groups=mesh['seq'=2,'section'=4,'tp'=4] {'seq'}, dimensions={0}, use_global_device_ids=true | all-gather | bytes 98304 | tf_op jit(solution)/shard_map/all_gather | solution.py:22
  367.9 4.4 %convolution_convert_fusion = bf16[64,4096]{1,0:T(8,128)(2,1)} fusion(bf16[64,512]{1,0:T(8,128)(2,1)S(1)} %convert_element_type.240, bf16[1,4096,512]{2,1,0:T(8,128)(2,1)} %all-gather.9.cloned.1.call-done), kind=kOutput, calls=%fused_computation.5 | convolution fusion | flops 268697600 | bytes 4784128 | tf_op jit(solution)/shard_map/dot_general | solution.py:93
  372.3 24.8 %reduce-scatter.11.cloned.1.call-done = bf16[64,1024]{1,0:T(8,128)(2,1)} async-done(((bf16[64,4096]{1,0:T(8,128)(2,1)}), bf16[64,1024]{1,0:T(8,128)(2,1)}) %reduce-scatter.11.cloned.1.call-update) | async-done | bytes 131088 | tf_op jit(solution)/shard_map/reduce_scatter | solution.py:96
  397.1 1.6 fusion.61
  (92 shorter events, 19.9 us)
Async XLA Ops:
  6.5 123.8 %all-gather.7.cloned.1.call-start = ((), (), s32[]{:S(2)}) async-start(), calls=%async_computation.5 | async-start | bytes 12582912 | tf_op jit(solution)/shard_map/all_gather | solution.py:122
  7.3 169.6 %all-gather.9.cloned.1.call-start = ((), (), s32[]{:S(2)}) async-start(), calls=%async_computation.6 | async-start | bytes 6291456 | tf_op jit(solution)/shard_map/all_gather | solution.py:123
  8.0 87.1 %copy-start.2 = (u32[32]{0:T(128)S(1)}, u32[32]{0:T(128)}, u32[]{:S(2)}) copy-start(u32[32]{0:T(128)} %constant.76) | copy-start | bytes 388
  8.0 88.4 %copy-start.1 = (s32[64]{0:T(128)S(1)}, s32[64]{0:T(128)}, u32[]{:S(2)}) copy-start(s32[64]{0:T(128)} %param.5) | copy-start | bytes 772
  8.0 100.7 %copy-start = (bf16[1,4096]{1,0:T(2,128)(2,1)S(1)}, bf16[1,4096]{1,0:T(2,128)(2,1)}, u32[]{:S(2)}) copy-start(bf16[1,4096]{1,0:T(2,128)(2,1)} %param.7) | copy-start | bytes 24580
  105.0 9.5 %all-to-all-start = ((bf16[512,2,64]{0,2,1:T(8,128)(2,1)}), bf16[512,2,64]{0,2,1:T(8,128)(2,1)S(1)}, u32[]{:S(2)}, u32[]{:S(2)}) async-start(bf16[512,2,64]{0,2,1:T(8,128)(2,1)} %broadcast_select_fusion), calls=%async_computation | async-start | bytes 262144 | tf_op jit(solution)/shard_map/all_to_all | solution.py:119
  108.4 94.9 %reduce-scatter.5.cloned.1.call-start = ((), (), s32[]{:S(2)}) async-start(), calls=%async_computation.7 | async-start | bytes 655360 | tf_op jit(solution)/shard_map/reduce_scatter | solution.py:96
  181.2 86.5 %reduce-scatter.7.cloned.1.call-start = ((), (), s32[]{:S(2)}) async-start(), calls=%async_computation.8 | async-start | bytes 655360 | tf_op jit(solution)/shard_map/reduce_scatter | solution.py:96
  204.2 2.3 collective-permute-start
  243.0 89.5 %reduce-scatter.9.cloned.1.call-start = ((), (), s32[]{:S(2)}) async-start(), calls=%async_computation.9 | async-start | bytes 655360 | tf_op jit(solution)/shard_map/reduce_scatter | solution.py:96
  268.7 2.3 collective-permute-start.1
  307.8 89.3 %reduce-scatter.11.cloned.1.call-start = ((), (), s32[]{:S(2)}) async-start(), calls=%async_computation.10 | async-start | bytes 655360 | tf_op jit(solution)/shard_map/reduce_scatter | solution.py:96
  333.5 2.3 collective-permute-start.2
Sparse Core Ops, SparseCore 0:
  8.9 108.1 all-gather.6
  118.6 58.1 all-gather.8
  181.4 21.8 reduce-scatter.4
  243.1 24.6 reduce-scatter.6
  307.9 24.6 reduce-scatter.8
  372.4 24.6 reduce-scatter.10
